TPU v7x, 256 devices: a whole 4x4x8 slice. The times are simulated.
256 devices in a mesh: seq: 256 (over x, y, z, core).
Axes of the slice: x: 4, y: 4, z: 8, core: 2. Of those that a mesh axis runs over, the one named last changes fastest.
Arguments:
- tokens: bfloat16 [131072, 1024], P('seq'), may hold values from -128 to 128, as said below
- w_query: bfloat16 [1024, 1024], replicated, may hold values from -0.1875 to 0.1875
- w_key: bfloat16 [1024, 256], replicated, may hold values from -0.1875 to 0.1875
- w_value: bfloat16 [1024, 256], replicated, may hold values from -0.1875 to 0.1875
- w_out: bfloat16 [1024, 1024], replicated, may hold values from -0.1875 to 0.1875
Outputs:
- attended: bfloat16 [131072, 1024], P('seq')
Inputs may be any that keep to these rules, and one draw needn't show every extreme that they name: `tokens`: Real-valued activations.
All inputs are finite; a program needn't handle non-finite values.
Results may differ from a plain program's by a relative error of at most 0.007.
The roundings to bfloat16 on the way count: a program that leaves them out, or rounds other values in their place, can miss the bound.
Values may be sent and summed in bfloat16 or wider, within the bound.
A program may use at most 128 MiB of HBM per device.

v0:
```python
import math

import jax
import jax.numpy as jnp
from jax import lax
from jax.sharding import PartitionSpec as P

HEADS = 16
KV_HEADS = 4
HEAD_DIM = 64
BLOCK = 256
POOL = 16
GROUP = 16


def extended(cells, sides, width):
    for axis, dim in sides:
        count = lax.axis_size(axis)
        ends = count - 1
        head = lax.slice_in_dim(cells, 0, width, axis=dim)
        tail = lax.slice_in_dim(cells, cells.shape[dim] - width, cells.shape[dim], axis=dim)
        cells = jnp.concatenate(
            [
                lax.ppermute(tail, axis, [(i, (i + 1) % count) for i in range(ends)]),
                cells,
                lax.ppermute(head, axis, [((i + 1) % count, i) for i in range(ends)]),
            ],
            axis=dim,
        )
    return cells


def from_partner(block, axis, apart):
    count = lax.axis_size(axis)
    route = []
    for low in range(count):
        high = low | 1 << apart
        if high != low and high < count:
            route += [(low, high), (high, low)]
    return lax.ppermute(block, axis, route)


def pool_rows(source, factor):
    width = source.shape[-1]
    grouped = source.astype(jnp.float32).reshape(-1, factor, width)
    return jnp.mean(grouped, axis=1).astype(jnp.bfloat16)


def usable_rows(block_index, my_group, all_blocks, group_tokens, group_summaries):
    near = block_index - 1 + jnp.arange(3 * BLOCK, dtype=jnp.int32) // BLOCK
    near_usable = (near >= 0) & (near < all_blocks)
    middle_blocks = (
        (my_group * group_summaries + jnp.arange(group_summaries, dtype=jnp.int32)) * POOL // BLOCK
    )
    middle_usable = jnp.abs(middle_blocks - block_index) > 1
    coarse_blocks = jnp.arange(all_blocks, dtype=jnp.int32)
    coarse_usable = (coarse_blocks * BLOCK // group_tokens != my_group) & (
        jnp.abs(coarse_blocks - block_index) > 1
    )
    return jnp.concatenate([near_usable, middle_usable, coarse_usable])


def attend_block(queries, pair_rows, usable):
    span_rows = pair_rows.shape[0]
    key_width = KV_HEADS * HEAD_DIM
    key_rows = pair_rows[:, :key_width].reshape(span_rows, KV_HEADS, HEAD_DIM)
    value_rows = pair_rows[:, key_width:].reshape(span_rows, KV_HEADS, HEAD_DIM)
    shaped = queries.reshape(-1, KV_HEADS, HEADS // KV_HEADS, HEAD_DIM)
    scores = jnp.einsum("qkgd,lkd->kgql", shaped, key_rows, preferred_element_type=jnp.float32) * (
        1.0 / math.sqrt(HEAD_DIM)
    )
    scores = jnp.where(usable, scores, -1e30)
    highest = jnp.max(scores, axis=-1, keepdims=True)
    weights = jnp.where(usable, jnp.exp(scores - highest), 0.0)
    totals = jnp.sum(weights, axis=-1)
    probabilities = weights.astype(jnp.bfloat16)
    weighted = jnp.einsum(
        "kgql,lkd->qkgd", probabilities, value_rows, preferred_element_type=jnp.float32
    )
    weighted = weighted / jnp.transpose(totals, (2, 0, 1))[..., None]
    return weighted.reshape(queries.shape[0], HEADS * HEAD_DIM).astype(jnp.bfloat16)


def body(tokens, w_query, w_key, w_value, w_out):
    devices = lax.axis_size("seq")
    my_index = lax.axis_index("seq")
    tok_rows = tokens.shape[0]
    block_count = tok_rows // BLOCK
    all_blocks = block_count * devices
    group_tokens = GROUP * tok_rows
    group_summaries = group_tokens // POOL
    queries = jnp.dot(tokens, w_query, preferred_element_type=jnp.float32).astype(jnp.bfloat16)
    key_rows = jnp.dot(tokens, w_key, preferred_element_type=jnp.float32).astype(jnp.bfloat16)
    value_rows = jnp.dot(tokens, w_value, preferred_element_type=jnp.float32).astype(jnp.bfloat16)
    pair_rows = jnp.concatenate([key_rows, value_rows], axis=1)
    padded = extended(pair_rows, (("seq", 0),), BLOCK)
    middle = pool_rows(pair_rows, POOL)
    coarse = pool_rows(pair_rows, BLOCK)
    my_group = my_index // GROUP
    group_mid = middle
    for level in range(GROUP.bit_length() - 1):
        partner = from_partner(group_mid, "seq", level)
        upper = my_index // 2**level % 2
        group_mid = jnp.where(
            upper == 1,
            jnp.concatenate([partner, group_mid], axis=0),
            jnp.concatenate([group_mid, partner], axis=0),
        )
    coarse_all = lax.all_gather(coarse, "seq", axis=0, tiled=True)

    def per_block(local_block):
        block_index = my_index * block_count + local_block
        near_rows = lax.dynamic_slice_in_dim(padded, local_block * BLOCK, 3 * BLOCK, 0)
        block_queries = lax.dynamic_slice_in_dim(queries, local_block * BLOCK, BLOCK, 0)
        gathered = jnp.concatenate([near_rows, group_mid, coarse_all], axis=0)
        usable = usable_rows(block_index, my_group, all_blocks, group_tokens, group_summaries)
        return attend_block(block_queries, gathered, usable)

    mixed = lax.map(per_block, jnp.arange(block_count, dtype=jnp.int32)).reshape(
        tok_rows, HEADS * HEAD_DIM
    )
    return jnp.dot(mixed, w_out, preferred_element_type=jnp.float32).astype(jnp.bfloat16)


def solution(mesh):
    placed = (P("seq", None), P(), P(), P(), P())
    return jax.shard_map(
        body, mesh=mesh, in_specs=placed, out_specs=P("seq", None), check_vma=False
    )
```

profile of v0, /device:TPU:1, one launch (start us, length us, event | category | flops | bytes accessed | tf_op | source)
XLA Modules:
  0.0 185.7 jit_solution(6386094796777122726)
XLA Ops:
  0.0 1.9 %convolution_convert_fusion.3 = bf16[512,256]{1,0:T(8,128)(2,1)S(1)} fusion(bf16[512,1024]{1,0:T(8,128)(2,1)} %param.7, bf16[1024,256]{1,0:T(8,128)(2,1)} %param.9), kind=kOutput, calls=%fused_computation.61 | convolution fusion | flops 268566528 | bytes 1835008 | tf_op jit(solution)/shard_map/dot_general | solution.py:93
  2.0 1.8 convolution_convert_fusion.2
  4.0 3.3 %collective-permute-start.2 = (bf16[32,512]{1,0:T(8,128)(2,1)S(1)}, bf16[32,512]{1,0:T(8,128)(2,1)S(1)}, u32[]{:S(2)}, u32[]{:S(2)}) collective-permute-start(bf16[32,512]{1,0:T(8,128)(2,1)S(1)} %multiply_convert_fusion), channel_id=1, source_target_pairs={{0,1},{1,0},{2,3},{3,2},{4,5},{5,4},{6,7},{7,6},{8,9},{9,8},{10,11... | collective-permute-start | bytes 98312 | tf_op jit(solution)/shard_map/ppermute | solution.py:40
  8.1 1.9 %collective-permute-start = (bf16[256,512]{1,0:T(8,128)(2,1)}, bf16[256,512]{1,0:T(8,128)(2,1)}, u32[]{:S(2)}, u32[]{:S(2)}) collective-permute-start(bf16[256,512]{1,0:T(8,128)(2,1)} %get-tuple-element.219), channel_id=1, source_target_pairs={{0,1},{1,2},{2,3},{3,4},{4,5},{5,6},{6,7},{7,8},{8,9},{9,10},{10,1... | collective-permute-start | bytes 786440 | tf_op jit(solution)/shard_map/ppermute | solution.py:24
  10.0 3.1 %collective-permute-start.1 = (bf16[256,512]{1,0:T(8,128)(2,1)}, bf16[256,512]{1,0:T(8,128)(2,1)}, u32[]{:S(2)}, u32[]{:S(2)}) collective-permute-start(bf16[256,512]{1,0:T(8,128)(2,1)} %get-tuple-element.220), channel_id=1, source_target_pairs={{1,0},{2,1},{3,2},{4,3},{5,4},{6,5},{7,6},{8,7},{9,8},{10,9},{11,1... | collective-permute-start | bytes 786440 | tf_op jit(solution)/shard_map/ppermute | solution.py:26
  13.5 3.5 %convolution_convert_fusion.1 = bf16[512,1024]{1,0:T(8,128)(2,1)} fusion(bf16[512,1024]{1,0:T(8,128)(2,1)} %param.7, bf16[1024,1024]{1,0:T(8,128)(2,1)S(1)} %copy-done), kind=kOutput, calls=%fused_computation.59 | convolution fusion | flops 1074266112 | bytes 4194304 | tf_op jit(solution)/shard_map/dot_general | solution.py:92
  17.1 4.3 %collective-permute-start.4 = (bf16[128,512]{1,0:T(8,128)(2,1)S(1)}, bf16[128,512]{1,0:T(8,128)(2,1)S(1)}, u32[]{:S(2)}, u32[]{:S(2)}) collective-permute-start(bf16[128,512]{1,0:T(8,128)(2,1)S(1)} %maximum_select_fusion.2), channel_id=1, source_target_pairs={{0,4},{4,0},{1,5},{5,1},{2,6},{6,2},{3,7},{7,3},{8,12},{12,8},{9,1... | collective-permute-start | bytes 393224 | tf_op jit(solution)/shard_map/ppermute | solution.py:40
  21.4 6.5 %collective-permute-done.4 = bf16[128,512]{1,0:T(8,128)(2,1)S(1)} collective-permute-done((bf16[128,512]{1,0:T(8,128)(2,1)S(1)}, bf16[128,512]{1,0:T(8,128)(2,1)S(1)}, u32[]{:S(2)}, u32[]{:S(2)}) %collective-permute-start.4) | collective-permute-done | bytes 131104 | tf_op jit(solution)/shard_map/ppermute | solution.py:40
  28.6 73.2 %all-gather = bf16[256,2,512]{2,1,0:T(2,128)(2,1)S(1)} all-gather(bf16[1,2,512]{2,1,0:T(2,128)(2,1)S(1)} %fusion.43), channel_id=1, replica_groups=mesh['seq'=256] {'seq'}, dimensions={0}, use_global_device_ids=true | all-gather | bytes 526336 | tf_op jit(solution)/shard_map/all_gather | solution.py:109
  102.8 2.1 %copy.17 = bf16[512,512]{0,1:T(8,128)(2,1)} copy(bf16[512,512]{1,0:T(8,128)(2,1)} %reshape.50) | data formatting | bytes 1048576 | tf_op jit(solution)/shard_map/while | solution.py:119
  104.8 2.1 %pad_maximum_fusion.1 = bf16[1024,512]{1,0:T(8,128)(2,1)} fusion(bf16[256,512]{1,0:T(8,128)(2,1)} %collective-permute-done.1, bf16[512,256]{1,0:T(8,128)(2,1)S(1)} %convolution_convert_fusion.2, bf16[512,256]{1,0:T(8,128)(2,1)S(1)} %convolution_convert_fusion.3, bf16[256,512]{1,0:T(8,128)(2,1)} %collective-permute-done), kind=kLoop, calls=%fused_computation.62 | loop fusion | flops 4194304 | bytes 2097152 | tf_op jit(solution)/shard_map/concatenate | solution.py:22
  106.9 1.2 maximum_select_fusion
  109.6 71.9 %while.13 = (s32[]{:T(128)}, bf16[2,256,1024]{2,1,0:T(8,128)(2,1)}, s32[2]{0:T(128)}, bf16[1024,512]{1,0:T(8,128)(2,1)}, bf16[512,512]{0,1:T(8,128)(2,1)}, /*ind...) while((s32[]{:T(128)}, bf16[2,256,1024]{2,1,0:T(8,128)(2,1)}, ...), condition=%wide.region_5.6_spmd, body=%wide.region_2.5_spmd.sunk | while | flops 1929153280 | bytes 46964504 | solution.py:119
  111.4 2.1 %constant_dynamic-slice_fusion.4 = bf16[768,512]{1,0:T(8,128)(2,1)} fusion(bf16[1024,512]{1,0:T(8,128)(2,1)} %get-tuple-element.331, s32[]{:T(128)S(6)} %select_n.189), kind=kLoop, calls=%fused_computation.54.clone.1 | loop fusion | bytes 1572868 | tf_op jit(solution)/shard_map/while/body/eval_jaxpr/dynamic_slice | solution.py:113
  113.4 1.4 copy.30
  114.8 1.3 pad_maximum_fusion.4
  119.9 16.8 %fusion.76 = (f32[4,4,256]{2,1,0:T(4,128)S(1)}, bf16[4,4,256,1792]{2,3,1,0:T(8,128)(2,1)}) fusion(pred[1792]{0:T(1024)(128)(4,1)S(1)} %pad_add_fusion.2, bf16[1792,4,64,1]{0,2,3,1:T(8,128)(2,1)} %bitcast.80, bf16[256,4,4,64]{0,3,2,1:T(8,128)(2,1)} %bitcast.81), kind=kOutput, calls=%fused_computation.77.clone.1 | convolution fusion | flops 983566080 | bytes 16140032 | tf_op jit(solution)/shard_map/while/body/eval_jaxpr/sub | solution.py:74
  136.7 7.8 %fusion.77 = bf16[256,4,4,64]{0,3,2,1:T(8,128)(2,1)S(1)} fusion(bf16[1792,4,64,1]{0,2,3,1:T(8,128)(2,1)S(1)} %bitcast.78, bf16[4,4,256,1792]{2,3,1,0:T(8,128)(2,1)} %get-tuple-element.294, f32[256,4,4]{0,2,1:T(4,128)S(1)} %bitcast.86), kind=kOutput, calls=%fused_computation.15.clone.1 | convolution fusion | flops 940048384 | bytes 16138240 | tf_op jit(solution)/shard_map/while/body/eval_jaxpr/kgql,lkd->qkgd/dot_general | solution.py:77
  147.3 2.1 %constant_dynamic-slice_fusion.4 = bf16[768,512]{1,0:T(8,128)(2,1)} fusion(bf16[1024,512]{1,0:T(8,128)(2,1)} %get-tuple-element.331, s32[]{:T(128)S(6)} %select_n.189), kind=kLoop, calls=%fused_computation.54.clone.1 | loop fusion | bytes 1572868 | tf_op jit(solution)/shard_map/while/body/eval_jaxpr/dynamic_slice | solution.py:113
  149.4 1.4 copy.30
  150.8 1.3 pad_maximum_fusion.4
  155.9 16.8 %fusion.76 = (f32[4,4,256]{2,1,0:T(4,128)S(1)}, bf16[4,4,256,1792]{2,3,1,0:T(8,128)(2,1)}) fusion(pred[1792]{0:T(1024)(128)(4,1)S(1)} %pad_add_fusion.2, bf16[1792,4,64,1]{0,2,3,1:T(8,128)(2,1)} %bitcast.80, bf16[256,4,4,64]{0,3,2,1:T(8,128)(2,1)} %bitcast.81), kind=kOutput, calls=%fused_computation.77.clone.1 | convolution fusion | flops 983566080 | bytes 16140032 | tf_op jit(solution)/shard_map/while/body/eval_jaxpr/sub | solution.py:74
  172.7 7.8 %fusion.77 = bf16[256,4,4,64]{0,3,2,1:T(8,128)(2,1)S(1)} fusion(bf16[1792,4,64,1]{0,2,3,1:T(8,128)(2,1)S(1)} %bitcast.78, bf16[4,4,256,1792]{2,3,1,0:T(8,128)(2,1)} %get-tuple-element.294, f32[256,4,4]{0,2,1:T(4,128)S(1)} %bitcast.86), kind=kOutput, calls=%fused_computation.15.clone.1 | convolution fusion | flops 940048384 | bytes 16138240 | tf_op jit(solution)/shard_map/while/body/eval_jaxpr/kgql,lkd->qkgd/dot_general | solution.py:77
  181.6 4.1 %convolution_convert_fusion = bf16[512,1024]{1,0:T(8,128)(2,1)} fusion(bf16[512,1024]{1,0:T(8,128)(2,1)} %bitcast.87, bf16[1024,1024]{1,0:T(8,128)(2,1)} %param.11), kind=kOutput, calls=%fused_computation.58 | convolution fusion | flops 1074266112 | bytes 4194304 | tf_op jit(solution)/shard_map/dot_general | solution.py:122
  (39 shorter events, 15.5 us)
Async XLA Ops:
  0.0 13.5 %copy-start = (bf16[1024,1024]{1,0:T(8,128)(2,1)S(1)}, bf16[1024,1024]{1,0:T(8,128)(2,1)}, u32[]{:S(2)}) copy-start(bf16[1024,1024]{1,0:T(8,128)(2,1)} %param.8) | copy-start | bytes 6291460
  4.0 9.1 %collective-permute-start.2 = (bf16[32,512]{1,0:T(8,128)(2,1)S(1)}, bf16[32,512]{1,0:T(8,128)(2,1)S(1)}, u32[]{:S(2)}, u32[]{:S(2)}) collective-permute-start(bf16[32,512]{1,0:T(8,128)(2,1)S(1)} %multiply_convert_fusion), channel_id=1, source_target_pairs={{0,1},{1,0},{2,3},{3,2},{4,5},{5,4},{6,7},{7,6},{8,9},{9,8},{10,11... | collective-permute-start | bytes 98312 | tf_op jit(solution)/shard_map/ppermute | solution.py:40
  8.1 96.8 %collective-permute-start = (bf16[256,512]{1,0:T(8,128)(2,1)}, bf16[256,512]{1,0:T(8,128)(2,1)}, u32[]{:S(2)}, u32[]{:S(2)}) collective-permute-start(bf16[256,512]{1,0:T(8,128)(2,1)} %get-tuple-element.219), channel_id=1, source_target_pairs={{0,1},{1,2},{2,3},{3,4},{4,5},{5,6},{6,7},{7,8},{8,9},{9,10},{10,1... | collective-permute-start | bytes 786440 | tf_op jit(solution)/shard_map/ppermute | solution.py:24
  10.0 94.9 %collective-permute-start.1 = (bf16[256,512]{1,0:T(8,128)(2,1)}, bf16[256,512]{1,0:T(8,128)(2,1)}, u32[]{:S(2)}, u32[]{:S(2)}) collective-permute-start(bf16[256,512]{1,0:T(8,128)(2,1)} %get-tuple-element.220), channel_id=1, source_target_pairs={{1,0},{2,1},{3,2},{4,3},{5,4},{6,5},{7,6},{8,7},{9,8},{10,9},{11,1... | collective-permute-start | bytes 786440 | tf_op jit(solution)/shard_map/ppermute | solution.py:26
  13.1 4.0 %collective-permute-start.3 = (bf16[64,512]{1,0:T(8,128)(2,1)S(1)}, bf16[64,512]{1,0:T(8,128)(2,1)S(1)}, u32[]{:S(2)}, u32[]{:S(2)}) collective-permute-start(bf16[64,512]{1,0:T(8,128)(2,1)S(1)} %maximum_select_fusion.3), channel_id=1, source_target_pairs={{0,2},{2,0},{1,3},{3,1},{4,6},{6,4},{5,7},{7,5},{8,10},{10,8},{9,1... | collective-permute-start | bytes 196616 | tf_op jit(solution)/shard_map/ppermute | solution.py:40
  17.1 10.8 %collective-permute-start.4 = (bf16[128,512]{1,0:T(8,128)(2,1)S(1)}, bf16[128,512]{1,0:T(8,128)(2,1)S(1)}, u32[]{:S(2)}, u32[]{:S(2)}) collective-permute-start(bf16[128,512]{1,0:T(8,128)(2,1)S(1)} %maximum_select_fusion.2), channel_id=1, source_target_pairs={{0,4},{4,0},{1,5},{5,1},{2,6},{6,2},{3,7},{7,3},{8,12},{12,8},{9,1... | collective-permute-start | bytes 393224 | tf_op jit(solution)/shard_map/ppermute | solution.py:40
  28.0 79.0 %collective-permute-start.5 = (bf16[256,512]{1,0:T(8,128)(2,1)S(1)}, bf16[256,512]{1,0:T(8,128)(2,1)}, u32[]{:S(2)}, u32[]{:S(2)}) collective-permute-start(bf16[256,512]{1,0:T(8,128)(2,1)S(1)} %maximum_select_fusion.1), channel_id=1, source_target_pairs={{0,8},{8,0},{1,9},{9,1},{2,10},{10,2},{3,11},{11,3},{4,12},{12,4},... | collective-permute-start | bytes 786440 | tf_op jit(solution)/shard_map/ppermute | solution.py:40
where the time goes:
time: 187 us; the launch traced here: 186 us
  blocking collectives  73.2 us (39%)
  matrix products  60.6 us (32%)
  local copies, waits for them, and re-layouts  22.2 us (12%)
  starting transfers between devices  13.6 us (7%)
  other arithmetic  7.19 us (4%)
  waiting for transfers between devices  6.51 us (3%)
  loops' own time  2.32 us (1%)
    all_gather x1, blocking collectives, body(): coarse_all = lax.all_gather(coarse, 'seq', axis=0, tiled=True)  73.2 us
    sub x2, matrix products, attend_block(): weights = jnp.where(usable, jnp.exp(scores - highest), 0.0)  33.7 us
    dot_general x2, matrix products, attend_block(): jnp.einsum('kgql,lkd->qkgd', probabilities, value_rows, preferred_element...  15.6 us
    ppermute x4, starting transfers between devices, from_partner(): return lax.ppermute(block, axis, route)  8.57 us
    dynamic_slice x4, local copies, waits for them, and re-layouts, per_block(): lax.dynamic_slice_in_dim(padded, local_block * BLOCK, 3 * BLOCK, 0)  6.95 us
    ppermute x4, waiting for transfers between devices, from_partner(): return lax.ppermute(block, axis, route)  6.51 us
    dynamic_slice x4, local copies, waits for them, and re-layouts, per_block(): lax.dynamic_slice_in_dim(queries, local_block * BLOCK, BLOCK, 0)  4.15 us
    dot_general x1, matrix products, body(): jnp.dot(mixed, w_out, preferred_element_type=jnp.float32)  4.14 us
  transfers between devices with their start and end apart: 6, of which 1 were waited for; matrix products, arithmetic and copies ran while one was open for 5% of the time, Pallas kernels for 0%

commit v1 on v0

v1 whole, which is shorter than its diff:
```python
import functools
import math

import jax
import jax.numpy as jnp
from jax import lax
from jax.experimental import pallas as pl
from jax.experimental.pallas import tpu as pltpu
from jax.sharding import PartitionSpec as P

HEADS = 16
KV_HEADS = 4
PER_KV = HEADS // KV_HEADS
HEAD_DIM = 64
BLOCK = 256
POOL = 16
GROUP = 16
CHIPS = GROUP // 2
COLUMNS = 16
TOK = 512
D = 1024
KVW = KV_HEADS * HEAD_DIM
NEAR = 3 * BLOCK
MID = 512
COARSE = 512
VROWS = HEAD_DIM + 16
C_EXP = math.log2(math.e) / math.sqrt(HEAD_DIM)
F32 = jnp.float32
BF16 = jnp.bfloat16
MESH = pl.DeviceIdType.MESH


def iota(shape, dim):
    return lax.broadcasted_iota(jnp.int32, shape, dim)


def dot(a, b):
    return jnp.dot(a, b, preferred_element_type=F32)


def kernel(devices, tok_hbm, wq_hbm, wk_hbm, wv_hbm, wo_hbm, out_ref,
           tok, wkv, wq, wo, near, mid, zc, zf, coarse, qt, kp, vt, acc, mx, mixt,
           load_sem, halo_s, halo_r, mid_s, mid_r, zc_s, zc_r, co_s, co_r, rel_s, rel_r):
    me = lax.axis_index("seq")
    core = lax.rem(me, 2)
    pos = lax.rem(me, GROUP)
    chip = lax.div(pos, 2)
    column = lax.div(me, GROUP)
    all_blocks = devices * 2

    def at(index):
        return (index,)

    loads = [
        pltpu.make_async_copy(tok_hbm, tok, load_sem.at[0]),
        pltpu.make_async_copy(wk_hbm, wkv.at[:, pl.ds(0, KVW)], load_sem.at[1]),
        pltpu.make_async_copy(wv_hbm, wkv.at[:, pl.ds(KVW, KVW)], load_sem.at[2]),
        pltpu.make_async_copy(wq_hbm, wq, load_sem.at[3]),
        pltpu.make_async_copy(wo_hbm, wo, load_sem.at[4]),
    ]
    for copy in loads:
        copy.start()

    def in_column(k):
        return column * GROUP + lax.rem(pos + k, GROUP)

    def across(k):
        return lax.rem(column + k, COLUMNS) * GROUP + pos

    following = lax.rem(me + 1, devices)
    previous = lax.rem(me + devices - 1, devices)
    partner = column * GROUP + chip * 2 + 1 - core

    barrier = pltpu.get_barrier_semaphore()

    def greet(k, _):
        pl.semaphore_signal(barrier, inc=1, device_id=at(in_column(k)), device_id_type=MESH)
        pl.semaphore_signal(barrier, inc=1, device_id=at(across(k)), device_id_type=MESH)
        return 0

    lax.fori_loop(1, GROUP, greet, 0)
    pl.semaphore_signal(barrier, inc=1, device_id=at(following), device_id_type=MESH)
    pl.semaphore_signal(barrier, inc=1, device_id=at(previous), device_id_type=MESH)

    for copy in loads[:3]:
        copy.wait()
    kv = dot(tok[...], wkv[...]).astype(BF16)
    near[pl.ds(BLOCK, TOK), :] = kv

    row, col = iota((32, TOK), 0), iota((32, TOK), 1)
    pool_mid = jnp.where(col // POOL == row, 1.0 / POOL, 0.0).astype(BF16)
    mid[core, chip] = dot(pool_mid, kv).astype(BF16)
    row, col = iota((16, TOK), 0), iota((16, TOK), 1)
    mine = jnp.zeros((16, 128), F32)
    for j in range(4):
        pool_coarse = jnp.where(col // BLOCK == row - 2 * j, 1.0 / BLOCK, 0.0).astype(BF16)
        mine += dot(pool_coarse, kv[:, j * 128:(j + 1) * 128])
    zc[pos] = mine[:8].astype(BF16)

    pl.semaphore_wait(barrier, 2 * GROUP)

    def zc_copy(k):
        return pltpu.make_async_remote_copy(
            src_ref=zc.at[pos], dst_ref=zc.at[pos], send_sem=zc_s.at[k], recv_sem=zc_r.at[k],
            device_id=at(in_column(k)), device_id_type=MESH)

    def halo_copy(which):
        src = near.at[pl.ds((2 - which) * BLOCK, BLOCK), :]
        dst = near.at[pl.ds(which * 3 * BLOCK, BLOCK), :]
        return pltpu.make_async_remote_copy(
            src_ref=src, dst_ref=dst, send_sem=halo_s.at[which], recv_sem=halo_r.at[which],
            device_id=at(previous if which else following), device_id_type=MESH)

    def mid_copy(k):
        target = column * GROUP + lax.rem(chip + k, CHIPS) * 2 + core
        return pltpu.make_async_remote_copy(
            src_ref=mid.at[core, chip], dst_ref=mid.at[core, chip],
            send_sem=mid_s.at[k], recv_sem=mid_r.at[k],
            device_id=at(target), device_id_type=MESH)

    def coarse_copy(k):
        return pltpu.make_async_remote_copy(
            src_ref=coarse.at[column], dst_ref=coarse.at[column],
            send_sem=co_s.at[k], recv_sem=co_r.at[k],
            device_id=at(across(k)), device_id_type=MESH)

    def each(copy_of, count, act):
        def step(k, _):
            getattr(copy_of(k), act)()
            return 0
        lax.fori_loop(1, count, step, 0)

    relay = pltpu.make_async_remote_copy(
        src_ref=mid.at[core], dst_ref=mid.at[core], send_sem=rel_s, recv_sem=rel_r,
        device_id=at(partner), device_id_type=MESH)

    each(zc_copy, GROUP, "start")
    halo_copy(0).start()
    halo_copy(1).start()
    each(mid_copy, CHIPS, "start")

    loads[3].wait()
    q = dot(tok[...], wq[...]).astype(BF16)
    for b in range(2):
        qt[b] = q[b * BLOCK:(b + 1) * BLOCK].T.reshape(HEADS, HEAD_DIM, BLOCK)

    def prepare(b, rows, span, usable):
        own = near[pl.ds(pl.multiple_of(BLOCK + b * BLOCK, BLOCK), 16), :][0:1, :KVW].astype(F32)
        ok_rows = usable(iota((span, 1), 0))
        ok_cols = usable(iota((1, span), 1))
        keys = jnp.where(ok_rows, rows[:, :KVW].astype(F32), own).astype(BF16)
        values = rows[:, KVW:].T.astype(F32)
        values = jnp.where(ok_cols, values, 0.0).astype(BF16)
        count = jnp.broadcast_to(jnp.where(ok_cols, 1.0, 0.0), (16, span)).astype(BF16)
        for kv_head in range(KV_HEADS):
            part = slice(kv_head * HEAD_DIM, (kv_head + 1) * HEAD_DIM)
            kp[kv_head, 0:span, :] = keys[:, part]
            vt[kv_head, 0:HEAD_DIM, 0:span] = values[part]
            vt[kv_head, HEAD_DIM:VROWS, 0:span] = count

    def attend(b, span, first, last):
        def per_kv(kv_head, _):
            keys = kp[kv_head, 0:span, :]
            values = vt[kv_head, :, 0:span]
            for g in range(PER_KV):
                h = kv_head * PER_KV + g
                scores = dot(keys, qt[b, h])
                highest = jnp.max(scores, axis=0, keepdims=True)
                if not first:
                    before = mx[b, h]
                    highest = jnp.maximum(highest, before)
                weights = jnp.exp2((scores - highest) * C_EXP).astype(BF16)
                total = dot(values, weights)
                if not first:
                    total += acc[b, h] * jnp.exp2((before - highest) * C_EXP)
                if last:
                    inverse = 1.0 / total[HEAD_DIM:HEAD_DIM + 1]
                    mixt[b, h] = (total[:HEAD_DIM] * inverse).astype(BF16)
                else:
                    acc[b, h] = total
                    mx[b, h] = highest
            return 0
        lax.fori_loop(0, KV_HEADS, per_kv, 0)

    def near_phase(b):
        block = me * 2 + b
        def usable(i):
            there = block - 1 + i // BLOCK
            return (there >= 0) & (there < all_blocks)
        start = pl.multiple_of(b * BLOCK, BLOCK)
        prepare(b, near[pl.ds(start, NEAR), :], NEAR, usable)
        attend(b, NEAR, True, False)

    def halo_wait(slot):
        pltpu.make_async_remote_copy(
            src_ref=near.at[pl.ds(BLOCK, BLOCK), :],
            dst_ref=near.at[pl.ds(pl.multiple_of(slot * 3 * BLOCK, BLOCK), BLOCK), :],
            send_sem=halo_s.at[slot], recv_sem=halo_r.at[slot],
            device_id=at(following), device_id_type=MESH).wait_recv()

    early = 1 - core
    halo_wait(early)
    near_phase(early)

    each(zc_copy, GROUP, "wait_recv")
    zf[...] = zc[...].astype(F32).reshape(GROUP * 8, 128)
    for r in range(2):
        for j in range(4):
            coarse[column, r * 16:(r + 1) * 16, j * 128:(j + 1) * 128] = (
                zf[pl.ds(2 * j + r, GROUP, stride=8), :].astype(BF16))
    each(coarse_copy, COLUMNS, "start")

    halo_wait(core)
    near_phase(core)

    each(mid_copy, CHIPS, "wait_recv")
    relay.start()
    relay.wait_recv()

    def mid_phase(b, _):
        block = me * 2 + b
        def usable(i):
            there = column * 32 + (i // 32 % CHIPS * 2 + i // 256) * 2 + i // POOL % 2
            return jnp.abs(there - block) > 1
        prepare(b, mid[...].reshape(MID, 2 * KVW), MID, usable)
        attend(b, MID, False, False)
        return 0

    lax.fori_loop(0, 2, mid_phase, 0)

    each(coarse_copy, COLUMNS, "wait_recv")
    loads[4].wait()

    def coarse_phase(b, _):
        block = me * 2 + b
        def usable(i):
            there = i // 32 * 32 + i % 16 * 2 + i // 16 % 2
            return (i // 32 != column) & (jnp.abs(there - block) > 1)
        prepare(b, coarse[...].reshape(COARSE, 2 * KVW), COARSE, usable)
        attend(b, COARSE, False, True)
        mixed = mixt[b].reshape(HEADS * HEAD_DIM, BLOCK).T
        out_ref[pl.ds(pl.multiple_of(b * BLOCK, BLOCK), BLOCK), :] = dot(mixed, wo[...]).astype(BF16)
        return 0

    lax.fori_loop(0, 2, coarse_phase, 0)

    each(zc_copy, GROUP, "wait_send")
    halo_copy(0).wait_send()
    halo_copy(1).wait_send()
    each(mid_copy, CHIPS, "wait_send")
    each(coarse_copy, COLUMNS, "wait_send")
    relay.wait_send()


def body(tokens, w_query, w_key, w_value, w_out):
    devices = lax.axis_size("seq")
    dma = pltpu.SemaphoreType.DMA
    return pl.pallas_call(
        functools.partial(kernel, devices),
        out_shape=jax.ShapeDtypeStruct((TOK, D), BF16),
        in_specs=[pl.BlockSpec(memory_space=pl.ANY)] * 5,
        out_specs=pl.BlockSpec(memory_space=pltpu.VMEM),
        scratch_shapes=[
            pltpu.VMEM((TOK, D), BF16),
            pltpu.VMEM((D, 2 * KVW), BF16),
            pltpu.VMEM((D, HEADS * HEAD_DIM), BF16),
            pltpu.VMEM((HEADS * HEAD_DIM, D), BF16),
            pltpu.VMEM((4 * BLOCK, 2 * KVW), BF16),
            pltpu.VMEM((2, CHIPS, TOK // POOL, 2 * KVW), BF16),
            pltpu.VMEM((GROUP, 8, 128), BF16),
            pltpu.VMEM((GROUP * 8, 128), F32),
            pltpu.VMEM((COLUMNS, 32, 2 * KVW), BF16),
            pltpu.VMEM((2, HEADS, HEAD_DIM, BLOCK), BF16),
            pltpu.VMEM((KV_HEADS, NEAR, HEAD_DIM), BF16),
            pltpu.VMEM((KV_HEADS, VROWS, NEAR), BF16),
            pltpu.VMEM((2, HEADS, VROWS, BLOCK), F32),
            pltpu.VMEM((2, HEADS, 1, BLOCK), F32),
            pltpu.VMEM((2, HEADS, HEAD_DIM, BLOCK), BF16),
            dma((5,)),
            dma((2,)), dma((2,)),
            dma((CHIPS,)), dma((CHIPS,)),
            dma((GROUP,)), dma((GROUP,)),
            dma((COLUMNS,)), dma((COLUMNS,)),
            dma, dma,
        ],
        compiler_params=pltpu.CompilerParams(
            collective_id=0, has_side_effects=True, vmem_limit_bytes=60 * 1024 * 1024),
    )(tokens, w_query, w_key, w_value, w_out)


def solution(mesh):
    placed = (P("seq", None), P(), P(), P(), P())
    return jax.shard_map(
        body, mesh=mesh, in_specs=placed, out_specs=P("seq", None), check_vma=False
    )
```

time: 187 us -> 65.9 us (0.35)
  blocking collectives: 73.2 us -> 0 us
  Pallas kernels: 0 us -> 63.5 us
  matrix products: 60.6 us -> 0 us
  local copies, waits for them, and re-layouts: 22.2 us -> 2.26 us
  starting transfers between devices: 13.6 us -> 0 us
  other arithmetic: 7.19 us -> 0 us
  waiting for transfers between devices: 6.51 us -> 0 us
  loops' own time: 2.32 us -> 0 us
    all_gather x1 -> x0, blocking collectives: 73.2 us -> none  [body(): coarse_all = lax.all_gather(coarse, 'seq', axis=0, tiled=True)]
    pallas_call x0 -> x1, Pallas kernels: none -> 63.5 us  [body(): pl.pallas_call(functools.partial(kernel, devices), out_shape=jax.ShapeDty...]
    sub x2 -> x0, matrix products: 33.7 us -> none  [attend_block(): weights = jnp.where(usable, jnp.exp(scores - highest), 0.0)]
    dot_general x6 -> x0, matrix products: 26.9 us -> none  [the longest x2 15.6 us: attend_block(): jnp.einsum('kgql,lkd->qkgd', probabilities, value_rows, preferred_element...]
    ppermute x6 -> x0, starting transfers between devices: 13.6 us -> none  [the longest x4 8.57 us: from_partner(): return lax.ppermute(block, axis, route)]
    dynamic_slice x10 -> x0, local copies, waits for them, and re-layouts: 13.4 us -> none  [the longest x4 6.95 us: per_block(): lax.dynamic_slice_in_dim(padded, local_block * BLOCK, 3 * BLOCK, 0)]
    ppermute x6 -> x0, waiting for transfers between devices: 6.51 us -> none  [the longest x4 6.51 us: from_partner(): return lax.ppermute(block, axis, route)]
    concatenate x6 -> x0, other arithmetic: 5.57 us -> none  [the longest x2 2.64 us: per_block(): gathered = jnp.concatenate([near_rows, group_mid, coarse_all], axis=0)]
  transfers between devices with their start and end apart: 6 -> 0, of which waited for: 1 -> 0; matrix products, arithmetic and copies ran while one was open for 5% -> 0% of each run, Pallas kernels for 0% -> 0%
where the time goes in v1:
time: 65.9 us; the launch traced here: 65.8 us
  Pallas kernels  63.5 us (96%)
  local copies, waits for them, and re-layouts  2.26 us (3%)
    pallas_call x1, Pallas kernels, body(): pl.pallas_call(functools.partial(kernel, devices), out_shape=jax.ShapeDty...  63.5 us
    unnamed x1, local copies, waits for them, and re-layouts  2.26 us

profile of v1, /device:TPU:1, one launch (start us, length us, event | category | flops | bytes accessed | tf_op | source)
XLA Modules:
  0.0 65.8 jit_solution(14030060411294019572)
XLA Ops:
  0.0 63.5 %shard_map.55 = bf16[512,1024]{1,0:T(8,128)(2,1)} custom-call(bf16[512,1024]{1,0:T(8,128)(2,1)} %tok_hbm.1, bf16[1024,1024]{1,0:T(8,128)(2,1)} %wq_hbm.1, bf16[1024,256]{1,0:T(8,128)(2,1)} %wk_hbm.1, bf16[1024,256]{1,0:T(8,128)(2,1)} %wv_hbm.1, bf16[1024,1024]{1,0:T(8,128)(2,1)} %wo_hbm.1), custom_call_target="tpu_custom_call" | custom-call | tf_op jit(solution)/shard_map/pallas_call | solution.py:258
  63.5 2.3 %copy.7 = bf16[512,1024]{1,0:T(8,128)(2,1)} copy(bf16[512,1024]{1,0:T(8,128)(2,1)} %shard_map.55) | data formatting | bytes 2097152

commit v2 on v1

v2 whole, which is shorter than its diff:
```python
import functools
import math

import jax
import jax.numpy as jnp
from jax import lax
from jax.experimental import pallas as pl
from jax.experimental.pallas import tpu as pltpu
from jax.sharding import PartitionSpec as P

HEADS = 16
KV_HEADS = 4
PER_KV = HEADS // KV_HEADS
HEAD_DIM = 64
BLOCK = 256
POOL = 16
GROUP = 16
CHIPS = GROUP // 2
COLUMNS = 16
TOK = 512
UNROLL = 8
PIECE = 128
D = 1024
KVW = KV_HEADS * HEAD_DIM
NEAR = 3 * BLOCK
MID = 512
COARSE = 512
VROWS = HEAD_DIM + 16
C_EXP = math.log2(math.e) / math.sqrt(HEAD_DIM)
F32 = jnp.float32
BF16 = jnp.bfloat16
MESH = pl.DeviceIdType.MESH


def iota(shape, dim):
    return lax.broadcasted_iota(jnp.int32, shape, dim)


def dot(a, b):
    return jnp.dot(a, b, preferred_element_type=F32)


def kernel(devices, tok_hbm, wq_hbm, wk_hbm, wv_hbm, out_ref,
           tok, wkv, wq, near, mid, zc, zf, coarse, qt, kp, vt, s0, s1, acc, mx, mixt,
           load_sem, halo_s, halo_r, mid_s, mid_r, zc_s, zc_r, co_s, co_r, rel_s, rel_r):
    me = lax.axis_index("seq")
    core = lax.rem(me, 2)
    pos = lax.rem(me, GROUP)
    chip = lax.div(pos, 2)
    column = lax.div(me, GROUP)
    all_blocks = devices * 2

    def at(index):
        return (index,)

    loads = [
        pltpu.make_async_copy(tok_hbm, tok, load_sem.at[0]),
        pltpu.make_async_copy(wk_hbm, wkv.at[:, pl.ds(0, KVW)], load_sem.at[1]),
        pltpu.make_async_copy(wv_hbm, wkv.at[:, pl.ds(KVW, KVW)], load_sem.at[2]),
        pltpu.make_async_copy(wq_hbm, wq, load_sem.at[3]),
    ]
    for copy in loads:
        copy.start()

    def in_column(k):
        return column * GROUP + lax.rem(pos + k, GROUP)

    def across(k):
        return lax.rem(column + k, COLUMNS) * GROUP + pos

    following = lax.rem(me + 1, devices)
    previous = lax.rem(me + devices - 1, devices)
    partner = column * GROUP + chip * 2 + 1 - core

    barrier = pltpu.get_barrier_semaphore()

    def greet(k, _):
        pl.semaphore_signal(barrier, inc=1, device_id=at(in_column(k)), device_id_type=MESH)
        pl.semaphore_signal(barrier, inc=1, device_id=at(across(k)), device_id_type=MESH)
        return 0

    lax.fori_loop(1, GROUP, greet, 0)
    pl.semaphore_signal(barrier, inc=1, device_id=at(following), device_id_type=MESH)
    pl.semaphore_signal(barrier, inc=1, device_id=at(previous), device_id_type=MESH)

    for copy in loads[:3]:
        copy.wait()
    kv = dot(tok[...], wkv[...]).astype(BF16)
    near[pl.ds(BLOCK, TOK), :] = kv

    row, col = iota((32, TOK), 0), iota((32, TOK), 1)
    pool_mid = jnp.where(col // POOL == row, 1.0 / POOL, 0.0).astype(BF16)
    mid[core, chip] = dot(pool_mid, kv).astype(BF16)
    row, col = iota((16, TOK), 0), iota((16, TOK), 1)
    mine = jnp.zeros((16, 128), F32)
    for j in range(4):
        pool_coarse = jnp.where(col // BLOCK == row - 2 * j, 1.0 / BLOCK, 0.0).astype(BF16)
        mine += dot(pool_coarse, kv[:, j * 128:(j + 1) * 128])
    zc[pos] = mine[:8].astype(BF16)

    pl.semaphore_wait(barrier, 2 * GROUP)

    def zc_copy(k):
        return pltpu.make_async_remote_copy(
            src_ref=zc.at[pos], dst_ref=zc.at[pos], send_sem=zc_s.at[k], recv_sem=zc_r.at[k],
            device_id=at(in_column(k)), device_id_type=MESH)

    def halo_copy(which):
        src = near.at[pl.ds((2 - which) * BLOCK, BLOCK), :]
        dst = near.at[pl.ds(which * 3 * BLOCK, BLOCK), :]
        return pltpu.make_async_remote_copy(
            src_ref=src, dst_ref=dst, send_sem=halo_s.at[which], recv_sem=halo_r.at[which],
            device_id=at(previous if which else following), device_id_type=MESH)

    def mid_copy(k):
        target = column * GROUP + lax.rem(chip + k, CHIPS) * 2 + core
        return pltpu.make_async_remote_copy(
            src_ref=mid.at[core, chip], dst_ref=mid.at[core, chip],
            send_sem=mid_s.at[k], recv_sem=mid_r.at[k],
            device_id=at(target), device_id_type=MESH)

    def coarse_copy(k):
        return pltpu.make_async_remote_copy(
            src_ref=coarse.at[column], dst_ref=coarse.at[column],
            send_sem=co_s.at[k], recv_sem=co_r.at[k],
            device_id=at(across(k)), device_id_type=MESH)

    def each(copy_of, count, act):
        def step(k, _):
            getattr(copy_of(k), act)()
            return 0
        lax.fori_loop(1, count, step, 0)

    relay = pltpu.make_async_remote_copy(
        src_ref=mid.at[core], dst_ref=mid.at[core], send_sem=rel_s, recv_sem=rel_r,
        device_id=at(partner), device_id_type=MESH)

    each(zc_copy, GROUP, "start")
    halo_copy(0).start()
    halo_copy(1).start()
    each(mid_copy, CHIPS, "start")

    loads[3].wait()
    q = dot(tok[...], wq[...]).astype(BF16)
    for b in range(2):
        qt[b] = q[b * BLOCK:(b + 1) * BLOCK].T.reshape(HEADS, HEAD_DIM, BLOCK)

    def prepare(at_row, span, rows_at, variants):
        for r in range(0, span, PIECE):
            rows = rows_at(r)
            keys, values = rows[:, :KVW], rows[:, KVW:].T
            for slot, usable, own in variants:
                slot_keys, slot_values, count = keys, values, jnp.ones((16, PIECE), BF16)
                if usable is not None:
                    ok_rows = usable(iota((PIECE, 1), 0) + r)
                    ok_cols = usable(iota((1, PIECE), 1) + r)
                    slot_keys = jnp.where(ok_rows, keys.astype(F32), own).astype(BF16)
                    slot_values = jnp.where(ok_cols, values.astype(F32), 0.0).astype(BF16)
                    count = jnp.broadcast_to(jnp.where(ok_cols, 1.0, 0.0), (16, PIECE)).astype(BF16)
                there = pl.ds(at_row + r, PIECE)
                for kv_head in range(KV_HEADS):
                    part = slice(kv_head * HEAD_DIM, (kv_head + 1) * HEAD_DIM)
                    kp[slot, kv_head, there, :] = slot_keys[:, part]
                    vt[slot, kv_head, 0:HEAD_DIM, there] = slot_values[part]
                    vt[slot, kv_head, HEAD_DIM:VROWS, there] = count

    def own_key(b):
        return near[BLOCK + b * BLOCK:BLOCK + b * BLOCK + 16, :KVW].astype(F32)[0:1]

    def attend(base, span, shared, first, last):
        items = 2 * HEADS

        def place(i):
            b, h = lax.div(i, HEADS), lax.rem(i, HEADS)
            return b, h, (0 if shared else b), lax.div(h, PER_KV)

        def step(ahead, s_ahead, now, s_now, highest):
            if ahead is not None:
                b, h, slot, kv_head = place(ahead)
                query = qt[b, h]
                top = None
            if now is not None:
                nb, nh, nslot, nkv = place(now)
                total = None
            for t in range(0, span, BLOCK):
                if ahead is not None:
                    scores = dot(kp[slot, kv_head, base + t:base + t + BLOCK, :], query)
                    s_ahead[t:t + BLOCK, :] = scores
                    peak = jnp.max(scores.reshape(BLOCK // 8, 8, BLOCK), axis=0)
                    top = peak if top is None else jnp.maximum(top, peak)
                if now is not None:
                    weights = jnp.exp2((s_now[t:t + BLOCK, :] - highest) * C_EXP).astype(BF16)
                    part = dot(vt[nslot, nkv, :, base + t:base + t + BLOCK], weights)
                    total = part if total is None else total + part
            if now is not None:
                if not first:
                    total += acc[nb, nh] * jnp.exp2((mx[nb, nh] - highest) * C_EXP)
                if last:
                    inverse = 1.0 / total[HEAD_DIM:HEAD_DIM + 1]
                    mixt[nb, nh] = (total[:HEAD_DIM] * inverse).astype(BF16)
                else:
                    acc[nb, nh] = total
                    mx[nb, nh] = highest
            if ahead is not None:
                result = jnp.max(top, axis=0, keepdims=True)
                return result if first else jnp.maximum(result, mx[b, h])
            return None

        def several(i, highest):
            for k in range(UNROLL):
                ahead = UNROLL * i + k + 1
                if k == UNROLL - 1:
                    ahead = jnp.minimum(ahead, items - 1)
                held, filled = (s0, s1) if k % 2 == 0 else (s1, s0)
                highest = step(ahead, filled, UNROLL * i + k, held, highest)
            return highest

        lax.fori_loop(0, items // UNROLL, several, step(0, s0, None, None, None))

    def share_column():
        each(zc_copy, GROUP, "wait_recv")
        zf[...] = zc[...].astype(F32).reshape(GROUP * 8, 128)
        for r in range(2):
            for j in range(4):
                coarse[column, r * 16:(r + 1) * 16, j * 128:(j + 1) * 128] = (
                    zf[pl.ds(2 * j + r, GROUP, stride=8), :].astype(BF16))
        each(coarse_copy, COLUMNS, "start")

    prepare(0, TOK, lambda r: near[BLOCK + r:BLOCK + r + PIECE, :], [(0, None, None)])
    attend(0, TOK, True, True, False)
    share_column()

    halo_copy(0).wait_recv()
    halo_copy(1).wait_recv()
    for b in range(2):
        beside = me * 2 + 3 * b - 1
        there = jnp.logical_and(beside >= 0, beside < all_blocks)
        prepare(TOK, BLOCK, lambda r, b=b: near[b * 3 * BLOCK + r:b * 3 * BLOCK + r + PIECE, :],
                [(b, lambda i, there=there: (i >= 0) & there, own_key(b))])
    attend(TOK, BLOCK, False, False, False)

    def prepare_mid(at_row, which):
        def usable_for(b):
            def usable(i):
                there = column * 32 + (i // 32 * 2 + which) * 2 + i // POOL % 2
                return jnp.abs(there - (me * 2 + b)) > 1
            return usable
        rows_at = lambda r: mid[which, r // 32:(r + PIECE) // 32].reshape(PIECE, 2 * KVW)
        prepare(at_row, MID // 2, rows_at, [(b, usable_for(b), own_key(b)) for b in range(2)])

    each(mid_copy, CHIPS, "wait_recv")
    relay.start()
    prepare_mid(0, core)
    relay.wait_recv()
    prepare_mid(MID // 2, 1 - core)
    attend(0, MID, False, False, False)

    each(coarse_copy, COLUMNS, "wait_recv")
    def usable_for(b):
        def usable(i):
            there = i // 32 * 32 + i % 16 * 2 + i // 16 % 2
            return (i // 32 != column) & (jnp.abs(there - (me * 2 + b)) > 1)
        return usable
    prepare(0, COARSE, lambda r: coarse[r // 32:(r + PIECE) // 32].reshape(PIECE, 2 * KVW),
            [(b, usable_for(b), own_key(b)) for b in range(2)])
    attend(0, COARSE, False, False, True)
    for b in range(2):
        out_ref[b * BLOCK:(b + 1) * BLOCK, :] = mixt[b].reshape(HEADS * HEAD_DIM, BLOCK).T

    each(zc_copy, GROUP, "wait_send")
    halo_copy(0).wait_send()
    halo_copy(1).wait_send()
    each(mid_copy, CHIPS, "wait_send")
    each(coarse_copy, COLUMNS, "wait_send")
    relay.wait_send()


def body(tokens, w_query, w_key, w_value, w_out):
    devices = lax.axis_size("seq")
    dma = pltpu.SemaphoreType.DMA
    mixed = pl.pallas_call(
        functools.partial(kernel, devices),
        out_shape=jax.ShapeDtypeStruct((TOK, D), BF16),
        in_specs=[pl.BlockSpec(memory_space=pltpu.HBM)] * 4,
        out_specs=pl.BlockSpec(memory_space=pltpu.VMEM),
        scratch_shapes=[
            pltpu.VMEM((TOK, D), BF16),
            pltpu.VMEM((D, 2 * KVW), BF16),
            pltpu.VMEM((D, HEADS * HEAD_DIM), BF16),
            pltpu.VMEM((4 * BLOCK, 2 * KVW), BF16),
            pltpu.VMEM((2, CHIPS, TOK // POOL, 2 * KVW), BF16),
            pltpu.VMEM((GROUP, 8, 128), BF16),
            pltpu.VMEM((GROUP * 8, 128), F32),
            pltpu.VMEM((COLUMNS, 32, 2 * KVW), BF16),
            pltpu.VMEM((2, HEADS, HEAD_DIM, BLOCK), BF16),
            pltpu.VMEM((2, KV_HEADS, NEAR, HEAD_DIM), BF16),
            pltpu.VMEM((2, KV_HEADS, VROWS, NEAR), BF16),
            pltpu.VMEM((TOK, BLOCK), F32),
            pltpu.VMEM((TOK, BLOCK), F32),
            pltpu.VMEM((2, HEADS, VROWS, BLOCK), F32),
            pltpu.VMEM((2, HEADS, 1, BLOCK), F32),
            pltpu.VMEM((2, HEADS, HEAD_DIM, BLOCK), BF16),
            dma((4,)),
            dma((2,)), dma((2,)),
            dma((CHIPS,)), dma((CHIPS,)),
            dma((GROUP,)), dma((GROUP,)),
            dma((COLUMNS,)), dma((COLUMNS,)),
            dma, dma,
        ],
        compiler_params=pltpu.CompilerParams(
            collective_id=0, has_side_effects=True, vmem_limit_bytes=40 * 1024 * 1024),
    )(*[pltpu.with_memory_space_constraint(x, pltpu.HBM) for x in (tokens, w_query, w_key, w_value)])
    return jnp.dot(mixed, w_out, preferred_element_type=F32).astype(BF16)


def solution(mesh):
    placed = (P("seq", None), P(), P(), P(), P())
    return jax.shard_map(
        body, mesh=mesh, in_specs=placed, out_specs=P("seq", None), check_vma=False
    )
```

time: 65.9 us -> 43.9 us (0.67)
  Pallas kernels: 63.5 us -> 41.6 us
  local copies, waits for them, and re-layouts: 2.26 us -> 0.01 us
  matrix products: 0 us -> 2.22 us
    pallas_call x1, Pallas kernels: 63.5 us -> 41.6 us  [body(): pl.pallas_call(functools.partial(kernel, devices), out_shape=jax.ShapeDty...]
    unnamed x1 -> x2, local copies, waits for them, and re-layouts: 2.26 us -> 0.01 us
    dot_general x0 -> x1, matrix products: none -> 2.22 us  [body(): return jnp.dot(mixed, w_out, preferred_element_type=F32).astype(BF16)]
where the time goes in v2:
time: 43.9 us; the launch traced here: 43.8 us
  Pallas kernels  41.6 us (95%)
  matrix products  2.22 us (5%)
    pallas_call x1, Pallas kernels, body(): pl.pallas_call(functools.partial(kernel, devices), out_shape=jax.ShapeDty...  41.6 us
    dot_general x1, matrix products, body(): return jnp.dot(mixed, w_out, preferred_element_type=F32).astype(BF16)  2.22 us

profile of v2, /device:TPU:1, one launch (start us, length us, event | category | flops | bytes accessed | tf_op | source)
XLA Modules:
  0.0 43.8 jit_solution(156995961081764032)
XLA Ops:
  0.0 0.0 copy-start
  0.0 41.6 %shard_map.55 = bf16[512,1024]{1,0:T(8,128)(2,1)S(1)} custom-call(bf16[512,1024]{1,0:T(8,128)(2,1)} %tok_hbm.1, bf16[1024,1024]{1,0:T(8,128)(2,1)} %wq_hbm.1, bf16[1024,256]{1,0:T(8,128)(2,1)} %wk_hbm.1, bf16[1024,256]{1,0:T(8,128)(2,1)} %wv_hbm.1), custom_call_target="tpu_custom_call" | custom-call | tf_op jit(solution)/shard_map/pallas_call | solution.py:281
  41.6 0.0 copy-done
  41.6 2.2 %convolution_convert_fusion = bf16[512,1024]{1,0:T(8,128)(2,1)} fusion(bf16[512,1024]{1,0:T(8,128)(2,1)S(1)} %shard_map.55, bf16[1024,1024]{1,0:T(8,128)(2,1)S(1)} %copy-done), kind=kOutput, calls=%fused_computation | convolution fusion | flops 1074266112 | bytes 4194304 | tf_op jit(solution)/shard_map/dot_general | solution.py:313
Async XLA Ops:
  0.0 41.6 %copy-start = (bf16[1024,1024]{1,0:T(8,128)(2,1)S(1)}, bf16[1024,1024]{1,0:T(8,128)(2,1)}, u32[]{:S(2)}) copy-start(bf16[1024,1024]{1,0:T(8,128)(2,1)} %param.9) | copy-start | bytes 6291460

commit v3 on v2

--- a/solution.py
+++ b/solution.py
@@ -230,15 +230,6 @@
     attend(0, TOK, True, True, False)
     share_column()
 
-    halo_copy(0).wait_recv()
-    halo_copy(1).wait_recv()
-    for b in range(2):
-        beside = me * 2 + 3 * b - 1
-        there = jnp.logical_and(beside >= 0, beside < all_blocks)
-        prepare(TOK, BLOCK, lambda r, b=b: near[b * 3 * BLOCK + r:b * 3 * BLOCK + r + PIECE, :],
-                [(b, lambda i, there=there: (i >= 0) & there, own_key(b))])
-    attend(TOK, BLOCK, False, False, False)
-
     def prepare_mid(at_row, which):
         def usable_for(b):
             def usable(i):
@@ -251,9 +242,18 @@
     each(mid_copy, CHIPS, "wait_recv")
     relay.start()
     prepare_mid(0, core)
+
+    halo_copy(0).wait_recv()
+    halo_copy(1).wait_recv()
+    for b in range(2):
+        beside = me * 2 + 3 * b - 1
+        there = jnp.logical_and(beside >= 0, beside < all_blocks)
+        prepare(TOK, BLOCK, lambda r, b=b: near[b * 3 * BLOCK + r:b * 3 * BLOCK + r + PIECE, :],
+                [(b, lambda i, there=there: (i >= 0) & there, own_key(b))])
+
     relay.wait_recv()
     prepare_mid(MID // 2, 1 - core)
-    attend(0, MID, False, False, False)
+    attend(0, MID + BLOCK, False, False, False)
 
     each(coarse_copy, COLUMNS, "wait_recv")
     def usable_for(b):
@@ -295,8 +295,8 @@
             pltpu.VMEM((2, HEADS, HEAD_DIM, BLOCK), BF16),
             pltpu.VMEM((2, KV_HEADS, NEAR, HEAD_DIM), BF16),
             pltpu.VMEM((2, KV_HEADS, VROWS, NEAR), BF16),
-            pltpu.VMEM((TOK, BLOCK), F32),
-            pltpu.VMEM((TOK, BLOCK), F32),
+            pltpu.VMEM((NEAR, BLOCK), F32),
+            pltpu.VMEM((NEAR, BLOCK), F32),
             pltpu.VMEM((2, HEADS, VROWS, BLOCK), F32),
             pltpu.VMEM((2, HEADS, 1, BLOCK), F32),
             pltpu.VMEM((2, HEADS, HEAD_DIM, BLOCK), BF16),

time: 43.9 us -> 41.6 us (0.948)
  Pallas kernels: 41.6 us -> 39.3 us
    pallas_call x1, Pallas kernels: 41.6 us -> 39.3 us  [body(): pl.pallas_call(functools.partial(kernel, devices), out_shape=jax.ShapeDty...]
where the time goes in v3:
time: 41.6 us
  Pallas kernels  39.3 us (94%)
  matrix products  2.22 us (5%)
    pallas_call x1, Pallas kernels, body(): pl.pallas_call(functools.partial(kernel, devices), out_shape=jax.ShapeDty...  39.3 us
    dot_general x1, matrix products, body(): return jnp.dot(mixed, w_out, preferred_element_type=F32).astype(BF16)  2.22 us

profile of v3, /device:TPU:1, one launch (start us, length us, event | category | flops | bytes accessed | tf_op | source)
XLA Modules:
  0.0 41.6 jit_solution(14731082973707365284)
XLA Ops:
  0.0 0.0 copy-start
  0.0 39.3 %shard_map.55 = bf16[512,1024]{1,0:T(8,128)(2,1)S(1)} custom-call(bf16[512,1024]{1,0:T(8,128)(2,1)} %tok_hbm.1, bf16[1024,1024]{1,0:T(8,128)(2,1)} %wq_hbm.1, bf16[1024,256]{1,0:T(8,128)(2,1)} %wk_hbm.1, bf16[1024,256]{1,0:T(8,128)(2,1)} %wv_hbm.1), custom_call_target="tpu_custom_call" | custom-call | tf_op jit(solution)/shard_map/pallas_call | solution.py:281
  39.3 0.0 copy-done
  39.3 2.2 %convolution_convert_fusion = bf16[512,1024]{1,0:T(8,128)(2,1)} fusion(bf16[512,1024]{1,0:T(8,128)(2,1)S(1)} %shard_map.55, bf16[1024,1024]{1,0:T(8,128)(2,1)S(1)} %copy-done), kind=kOutput, calls=%fused_computation | convolution fusion | flops 1074266112 | bytes 4194304 | tf_op jit(solution)/shard_map/dot_general | solution.py:313
Async XLA Ops:
  0.0 39.3 %copy-start = (bf16[1024,1024]{1,0:T(8,128)(2,1)S(1)}, bf16[1024,1024]{1,0:T(8,128)(2,1)}, u32[]{:S(2)}) copy-start(bf16[1024,1024]{1,0:T(8,128)(2,1)} %param.9) | copy-start | bytes 6291460
